TPU v7x, 32 devices: a whole 2x2x4 slice. The times are simulated.
32 devices in a mesh: rep: 2 (over y), exp: 4 (over x, core), tp: 4 (over z).
Axes of the slice: x: 2, y: 2, z: 4, core: 2. Of those that a mesh axis runs over, the one named last changes fastest.
Arguments:
- tokens: bfloat16 [256, 6144], P(('rep', 'exp'), 'tp'), parts along dimension 0, may hold values from -6 to 6
- expert_ids: int32 [256, 2], P(('rep', 'exp')), parts along dimension 0, may hold values from 0 to 3, all different within a row; in each aligned block of 32 rows (0 to 31, 32 to 63, ...) at most 20 rows name the same one
- route_logits: float32 [256, 2], P(('rep', 'exp')), parts along dimension 0, may hold values from -6 to 6
- gate_weight: bfloat16 [6144, 32768], P(None, ('exp', 'tp')), may hold values from -0.078125 to 0.078125
- up_weight: bfloat16 [6144, 32768], P(None, ('exp', 'tp')), may hold values from -0.078125 to 0.078125
- down_weight: bfloat16 [32768, 6144], P(('exp', 'tp')), may hold values from -0.0625 to 0.0625
Outputs:
- moe_out: bfloat16 [256, 6144], P(('rep', 'exp'), 'tp'), parts along dimension 0
There are 2 independent parts, one for each index of `rep`. A program takes and returns all parts, laid end to end along the dimension named above; an argument that names none is the same for every part. Nothing has to cross between parts.
Inputs may be any that keep to these rules, and one draw needn't show every extreme that they name: `expert_ids`: each token names two different experts. In each aligned block of 32 tokens no expert is named by more than 20 tokens, a bound that some block reaches.
All inputs are finite; a program needn't handle non-finite values.
Results may differ from a plain program's by a relative error of at most 0.019.
Values may be sent and summed in bfloat16 or wider, within the bound.
A program may use at most 128 MiB of HBM per device.

v0:
```python
import functools

import jax
import jax.numpy as jnp
from jax import lax
from jax.experimental import pallas as pl
from jax.experimental.pallas import tpu as pltpu
from jax.sharding import PartitionSpec as P

EXPERTS = 4
CORES = 2
MESH = pl.DeviceIdType.MESH
F32 = jnp.float32
BF16 = jnp.bfloat16


def near_first(n):
    order = [0]
    for d in range(1, n // 2 + 1):
        for v in (d, n - d):
            if v not in order:
                order.append(v)
    return order


def tile_of(n):
    return next(t for t in (512, 384, 256, 128) if n % t == 0)


def kernel(
    n_exp,
    n_tp,
    n_w,
    tok_ref,
    ids_ref,
    log_ref,
    gate_hbm,
    up_hbm,
    down_hbm,
    out_ref,
    gate_w,
    up_w,
    down_w,
    rows,
    acc_g,
    acc_u,
    hidden,
    share,
    wcol,
    psend,
    precv,
    comb,
    xrecv,
    zsend,
    zrecv,
    gate_sem,
    up_sem,
    down_sem,
    in_z,
    in_x,
    in_p,
    share_x,
    share_p,
    out_p,
    out_x,
    out_z,
):
    n_x = n_exp // CORES
    tok, dc = tok_ref.shape
    width = acc_g.shape[1]
    half = n_x * tok
    me = lax.axis_index("exp")
    z = lax.axis_index("tp")
    x = me // CORES
    core = me % CORES
    partner = x * CORES + (1 - core)
    peers = [lax.rem(x + k, n_x) for k in range(1, n_x)]
    order = near_first(n_tp)
    out_order = order[::-1]
    mine = pl.ds(pl.multiple_of(x * tok, tok), tok)

    def remote(src, dst, sems, idx, device):
        return pltpu.make_async_remote_copy(
            src_ref=src,
            dst_ref=dst,
            send_sem=sems.at[(0,) + idx],
            recv_sem=sems.at[(1,) + idx],
            device_id=device,
            device_id_type=MESH,
        )

    def load_in(i):
        f = lax.rem(z + order[i], n_tp)
        r = pl.ds(pl.multiple_of(f * dc, dc), dc)
        s = i % n_w
        return (
            pltpu.make_async_copy(gate_hbm.at[r, :], gate_w.at[s], gate_sem.at[s]),
            pltpu.make_async_copy(up_hbm.at[r, :], up_w.at[s], up_sem.at[s]),
        )

    def load_down(i):
        f = lax.rem(z + out_order[i], n_tp)
        c = pl.ds(pl.multiple_of(f * dc, dc), dc)
        s = i % n_w
        return pltpu.make_async_copy(down_hbm.at[:, c], down_w.at[s], down_sem.at[s])

    for i in range(n_w):
        for c in load_in(i):
            c.start()

    barrier = pltpu.get_barrier_semaphore()
    pl.semaphore_signal(barrier, inc=1, device_id={"exp": partner}, device_id_type=MESH)
    for p in peers:
        pl.semaphore_signal(
            barrier, inc=1, device_id={"exp": p * CORES + core}, device_id_type=MESH
        )
    for d in range(1, n_tp):
        pl.semaphore_signal(
            barrier, inc=1, device_id={"tp": lax.rem(z + d, n_tp)}, device_id_type=MESH
        )

    rows[0, mine, :] = tok_ref[...]
    lane = lax.broadcasted_iota(jnp.int32, (tok, 128), 1)
    eye = lax.broadcasted_iota(jnp.int32, (tok, tok), 0) == lax.broadcasted_iota(
        jnp.int32, (tok, tok), 1
    )

    def column(row):
        spread = jnp.where(eye, jnp.broadcast_to(row, (tok, tok)), jnp.zeros_like(row))
        return jnp.sum(spread, axis=1, keepdims=True)

    diff = column(log_ref[0:1, :] - log_ref[1:2, :])
    ids = ids_ref[...].astype(F32)
    lane = lane.astype(F32)
    share[0, x] = jnp.where(column(ids[0:1]) == lane, jax.nn.sigmoid(diff), 0.0) + jnp.where(
        column(ids[1:2]) == lane, jax.nn.sigmoid(-diff), 0.0
    )
    pl.semaphore_wait(barrier, 1 + (n_x - 1) + (n_tp - 1))

    sends = []

    def send(copy):
        copy.start()
        sends.append(copy)
        return copy

    z_in = [None] + [
        send(
            remote(
                tok_ref,
                rows.at[i, mine, :],
                in_z,
                (i,),
                {"tp": lax.rem(z + n_tp - order[i], n_tp)},
            )
        )
        for i in range(1, n_tp)
    ]
    x_in = {}

    def send_x(i):
        if i >= n_tp:
            return
        if i > 0:
            z_in[i].wait_recv()
        src = tok_ref if i == 0 else rows.at[i, mine, :]
        x_in[i] = [
            send(
                remote(
                    src, rows.at[i, mine, :], in_x, (i, k), {"exp": p * CORES + core}
                )
            )
            for k, p in enumerate(peers)
        ]

    send_x(0)
    send_x(1)
    tn = tile_of(width)
    share_in = None
    relays = {}

    def relay_rows(i):
        if i >= n_tp:
            return
        for c in x_in[i]:
            c.wait_recv()
        relays[i] = send(
            remote(
                rows.at[i, pl.ds(0, half), :],
                rows.at[i, pl.ds(half, half), :],
                in_p,
                (i,),
                {"exp": partner},
            )
        )
        send_x(i + 2)

    relay_rows(0)
    for i in range(n_tp):
        if i == n_tp - 1:
            share_in = [
                send(
                    remote(
                        share.at[0, x], share.at[0, x], share_x, (k,), {"exp": p * CORES + core}
                    )
                )
                for k, p in enumerate(peers)
            ]
        relays[i].wait_recv()
        for c in load_in(i):
            c.wait()
        s = i % n_w

        def expert_in(t, i=i, s=s):
            cols = pl.ds(pl.multiple_of(t * tn, tn), tn)
            a = rows[i]
            g = jnp.dot(a, gate_w[s, :, cols], preferred_element_type=F32)
            u = jnp.dot(a, up_w[s, :, cols], preferred_element_type=F32)
            if i > 0:
                g = g + acc_g[:, cols]
                u = u + acc_u[:, cols]
            if i < n_tp - 1:
                acc_g[:, cols] = g
                acc_u[:, cols] = u
            else:
                hidden[:, cols] = (g * jax.nn.sigmoid(g) * u).astype(BF16)

        middle = width // tn // 2
        if middle:
            pl.loop(0, middle)(expert_in)
        relay_rows(i + 1)
        pl.loop(middle, width // tn)(expert_in)

        if i + n_w < n_tp:
            for c in load_in(i + n_w):
                c.start()
        if i == max(n_tp - n_w - 1, 0):
            for j in range(n_w):
                load_down(j).start()

    for c in share_in:
        c.wait_recv()
    share_relay = send(
        remote(share.at[0], share.at[1], share_p, (0,), {"exp": partner})
    )
    share_relay.wait_recv()
    groups = n_exp // EXPERTS
    expert = me // groups
    lanes = lax.broadcasted_iota(jnp.int32, (CORES * half, 128), 1)
    wall = share[...].reshape(CORES * half, 128)
    wcol[...] = jnp.broadcast_to(
        jnp.sum(jnp.where(lanes == expert, wall, 0.0), axis=1, keepdims=True), wcol.shape
    )

    to = tile_of(dc)
    to_partner = {}
    to_x = {}
    to_z = {}

    def compute(i):
        load_down(i).wait()
        s = i % n_w

        @pl.loop(0, dc // to)
        def _(t):
            cols = pl.ds(pl.multiple_of(t * to, to), to)
            p = jnp.dot(hidden[...], down_w[s, :, cols], preferred_element_type=F32)
            p = p * wcol[:, 0:1]
            comb[i, :, cols] = p[:half].astype(BF16)
            psend[i, :, cols] = p[half:].astype(BF16)

        if i + n_w < n_tp:
            load_down(i + n_w).start()
        to_partner[i] = send(
            remote(psend.at[i], precv.at[i], out_p, (i,), {"exp": partner})
        )

    def combine(i):
        to_partner[i].wait_recv()
        comb[i] = (comb[i].astype(F32) + precv[i].astype(F32)).astype(BF16)
        to_x[i] = [
            send(
                remote(
                    comb.at[i, pl.ds(pl.multiple_of(p * tok, tok), tok), :],
                    xrecv.at[i, k],
                    out_x,
                    (i, k),
                    {"exp": p * CORES + core},
                )
            )
            for k, p in enumerate(peers)
        ]

    def home(i):
        total = comb[i, mine, :].astype(F32)
        for k, c in enumerate(to_x[i]):
            c.wait_recv()
            total = total + xrecv[i, k].astype(F32)
        d = out_order[i]
        if d == 0:
            return total
        zsend[i] = total.astype(BF16)
        to_z[i] = send(
            remote(zsend.at[i], zrecv.at[i], out_z, (i,), {"tp": lax.rem(z + d, n_tp)})
        )

    own = None
    lag = 3
    for i in range(n_tp + lag):
        if i < n_tp:
            compute(i)
        if 0 <= i - 1 < n_tp:
            combine(i - 1)
        if 0 <= i - lag < n_tp:
            r = home(i - lag)
            own = r if r is not None else own
    for i in to_z:
        to_z[i].wait_recv()
        own = own + zrecv[i].astype(F32)
    out_ref[...] = own.astype(BF16)
    for c in sends:
        c.wait_send()


def on_device(tokens, expert_ids, route_logits, gate_weight, up_weight, down_weight):
    n_exp = lax.axis_size("exp")
    n_tp = lax.axis_size("tp")
    n_x = n_exp // CORES
    tok, dc = tokens.shape
    width = gate_weight.shape[1]
    n_w = min(n_tp, 3)
    total = n_exp * tok
    half = n_x * tok
    dma = pltpu.SemaphoreType.DMA
    vmem = pl.BlockSpec(memory_space=pltpu.VMEM)
    hbm = pl.BlockSpec(memory_space=pl.ANY)
    return pl.pallas_call(
        functools.partial(kernel, n_exp, n_tp, n_w),
        out_shape=jax.ShapeDtypeStruct((tok, dc), BF16),
        in_specs=[vmem, vmem, vmem, hbm, hbm, hbm],
        out_specs=vmem,
        scratch_shapes=[
            pltpu.VMEM((n_w, dc, width), BF16),
            pltpu.VMEM((n_w, dc, width), BF16),
            pltpu.VMEM((n_w, width, dc), BF16),
            pltpu.VMEM((n_tp, total, dc), BF16),
            pltpu.VMEM((total, width), F32),
            pltpu.VMEM((total, width), F32),
            pltpu.VMEM((total, width), BF16),
            pltpu.VMEM((CORES, n_x, tok, 128), F32),
            pltpu.VMEM((total, 128), F32),
            pltpu.VMEM((n_tp, half, dc), BF16),
            pltpu.VMEM((n_tp, half, dc), BF16),
            pltpu.VMEM((n_tp, half, dc), BF16),
            pltpu.VMEM((n_tp, n_x - 1, tok, dc), BF16),
            pltpu.VMEM((n_tp, tok, dc), BF16),
            pltpu.VMEM((n_tp, tok, dc), BF16),
            dma((n_w,)),
            dma((n_w,)),
            dma((n_w,)),
            dma((2, n_tp)),
            dma((2, n_tp, n_x - 1)),
            dma((2, n_tp)),
            dma((2, n_x - 1)),
            dma((2, 1)),
            dma((2, n_tp)),
            dma((2, n_tp, n_x - 1)),
            dma((2, n_tp)),
        ],
        compiler_params=pltpu.CompilerParams(
            collective_id=0, has_side_effects=True, vmem_limit_bytes=67043328
        ),
    )(tokens, expert_ids.T, route_logits.T, gate_weight, up_weight, down_weight)


def solution(mesh):
    return jax.shard_map(
        on_device,
        mesh=mesh,
        in_specs=(
            P(("rep", "exp"), "tp"),
            P(("rep", "exp"), None),
            P(("rep", "exp"), None),
            P(None, ("exp", "tp")),
            P(None, ("exp", "tp")),
            P(("exp", "tp"), None),
        ),
        out_specs=P(("rep", "exp"), "tp"),
        check_vma=False,
    )
```

profile of v0, /device:TPU:0, one launch (start us, length us, event | category | flops | bytes accessed | tf_op | source)
XLA Modules:
  0.0 50.5 jit_solution(13249063887417911783)
XLA Ops:
  0.0 48.9 %shard_map.64 = bf16[32,1536]{1,0:T(8,128)(2,1)} custom-call(bf16[32,1536]{1,0:T(8,128)(2,1)} %tok_ref.1, s32[2,32]{1,0:T(2,128)} %bitcast.2, f32[2,32]{1,0:T(2,128)} %bitcast.3, bf16[6144,2048]{1,0:T(8,128)(2,1)} %gate_hbm.1, bf16[6144,2048]{1,0:T(8,128)(2,1)} %up_hbm.1, bf16[2048,6144]{1,0:T(8,128)(2,1)} %down_hbm.1), custom_call_target="tpu_custom_call" | custom-call | tf_op jit(solution)/shard_map/pallas_call | solution.py:337
  49.0 1.5 %copy.8 = bf16[32,1536]{1,0:T(8,128)(2,1)} copy(bf16[32,1536]{1,0:T(8,128)(2,1)} %shard_map.64) | data formatting | bytes 196608
where the time goes:
time: 50.7 us; the launch traced here: 50.5 us
  Pallas kernels  48.9 us (96%)
  local copies, waits for them, and re-layouts  1.54 us (3%)
    pallas_call x1, Pallas kernels, on_device(): pl.pallas_call(functools.partial(kernel, n_exp, n_tp, n_w), out_shape=jax...  48.9 us
    unnamed x1, local copies, waits for them, and re-layouts  1.54 us

commit v1 on v0

v1 whole, which is shorter than its diff:
```python
import functools

import jax
import jax.numpy as jnp
from jax import lax
from jax.experimental import pallas as pl
from jax.experimental.pallas import tpu as pltpu
from jax.sharding import PartitionSpec as P

EXPERTS = 4
CORES = 2
MESH = pl.DeviceIdType.MESH
F32 = jnp.float32
BF16 = jnp.bfloat16
RING_BYTES = 52 * 1000 * 1000
LAG_PAIR = 2
LAG_HOME = 6
LAG_GATE = 10


class Plan:
    def __init__(self, n_exp, n_tp, tok, dc, width):
        self.n_exp, self.n_tp, self.tok, self.dc, self.width = n_exp, n_tp, tok, dc, width
        self.n_x = n_exp // CORES
        self.h = n_tp // 2
        self.half = self.n_x * tok
        self.lanes = next(t for t in (512, 256, 128) if width % t == 0 and dc % t == 0)
        self.nt = width // self.lanes
        self.group = 2 if self.nt % 2 == 0 else 1
        self.pw = self.lanes if dc > 512 else dc
        self.nq = dc // self.pw
        self.n_pc = n_tp * self.nq
        self.cuts = 2 if tok % 32 == 0 and tok * dc >= 32768 else 1
        self.cut = tok // self.cuts
        loads = []
        steps = self.nt // self.group
        for i in range(n_tp):
            for t in range(self.nt):
                for kind in ("gate", "up"):
                    loads.append((kind, i, t, dc, i * steps + t // self.group))
        for pc in range(self.n_pc):
            i = n_tp - 1 - pc // self.nq
            for t in range(self.pw // self.lanes):
                tile = (pc % self.nq) * (self.pw // self.lanes) + t
                loads.append(("down", i, tile, width, n_tp * steps + pc))
        total = sum(l[3] for l in loads)
        self.rows = min(total, RING_BYTES // (2 * self.lanes) // 16 * 16)
        self.loads, live, head, last = [], [], 0, 0
        for kind, i, t, n, step in loads:
            if head + n > self.rows:
                head = 0
            hit = [l for l in live if l[0] < head + n and head < l[1]]
            last = max([last] + [l[2] + 1 for l in hit])
            assert last <= step
            live = [l for l in live if l not in hit] + [(head, head + n, step)]
            self.loads.append((kind, i, t, n, head, last))
            head += n
        self.at = {l[:3]: n for n, l in enumerate(self.loads)}


def kernel(
    pn,
    tok_hbm,
    ids_hbm,
    log_hbm,
    gate_hbm,
    up_hbm,
    down_hbm,
    out_ref,
    ring,
    rows,
    ids_v,
    log_v,
    shr,
    wcol,
    acc_g,
    acc_u,
    hidden,
    pown,
    psend,
    precv,
    xsend,
    xrecv,
    zsend,
    grecv,
    zrecv,
    gsum,
    own,
    w_sem,
    t_sem,
    rz,
    rx,
    rd,
    s_own,
    s_cross,
    s_fwd,
    sx,
    sd,
    share_x,
    share_d,
    pair2,
    x2,
    sz2,
    rg2,
    rz2,
):
    n_x, n_tp, h, tok, dc = pn.n_x, pn.n_tp, pn.h, pn.tok, pn.dc
    half, nq, lanes, pw = pn.half, pn.nq, pn.lanes, pn.pw
    me = lax.axis_index("exp")
    z = lax.axis_index("tp")
    x = me // CORES
    core = me % CORES
    partner = {"exp": x * CORES + (1 - core)}
    slot = [x] + [lax.rem(x + k, n_x) for k in range(1, n_x)]
    peers = [{"exp": p * CORES + core} for p in slot[1:]]
    side = z // h
    m = z + side * (n_tp - 1 - 2 * z)
    gate = m == h - 1
    member = m != h - 1

    def along(j):
        return {"tp": j + side * (n_tp - 1 - 2 * j)}

    def chunk(i):
        return lax.rem(m + i, h) if i < h else i

    def feature(i):
        return along(chunk(i))["tp"]

    def span(p):
        return pl.ds(pl.multiple_of(p * tok, tok), tok)

    def part(p, c):
        return pl.ds(pl.multiple_of(p * tok + c * pn.cut, pn.cut), pn.cut)

    def remote(src, dst, send, recv, device):
        return pltpu.make_async_remote_copy(
            src_ref=src,
            dst_ref=dst,
            send_sem=send,
            recv_sem=recv,
            device_id=device,
            device_id_type=MESH,
        )

    def load(n):
        kind, i, t, size, at, _ = pn.loads[n]
        f = feature(i)
        if kind == "down":
            c = pl.ds(pl.multiple_of(f * dc + t * lanes, lanes), lanes)
            src = down_hbm.at[:, c]
        else:
            r = pl.ds(pl.multiple_of(f * dc, dc), dc)
            hbm = gate_hbm if kind == "gate" else up_hbm
            src = hbm.at[r, pl.ds(t * lanes, lanes)]
        return pltpu.make_async_copy(src, ring.at[pl.ds(at, size), :], w_sem.at[n])

    def tile(kind, i, t):
        size, at = pn.loads[pn.at[kind, i, t]][3:5]
        return ring[at : at + size, :]

    def start_loads(step):
        for n, l in enumerate(pn.loads):
            if l[5] == step:
                load(n).start()

    sends, gate_sends, member_sends = [], [], []

    def send(copy, log=sends):
        copy.start()
        log.append(copy)

    barrier = pltpu.get_barrier_semaphore()

    def signal(device):
        pl.semaphore_signal(barrier, inc=1, device_id=device, device_id_type=MESH)

    first = [
        pltpu.make_async_copy(ids_hbm, ids_v, t_sem.at[0]),
        pltpu.make_async_copy(log_hbm, log_v, t_sem.at[1]),
        pltpu.make_async_copy(tok_hbm, rows.at[0, span(x), :], t_sem.at[2]),
    ]
    for c in first:
        c.start()
    signal(partner)
    for p in peers:
        signal(p)
    for k in range(1, h):
        signal(along(lax.rem(m + k, h)))
    signal(along(h))

    @pl.when(gate)
    def _():
        for j in range(h + 1, n_tp):
            signal(along(j))

    start_loads(0)

    first[0].wait()
    first[1].wait()
    diff = log_v[0:1, :] - log_v[1:2, :]
    to_first, to_second = jax.nn.sigmoid(diff), jax.nn.sigmoid(-diff)
    for e in range(EXPERTS):
        shr[0, x, e : e + 1, 0:tok] = jnp.where(ids_v[0:1, :] == e, to_first, 0.0) + jnp.where(
            ids_v[1:2, :] == e, to_second, 0.0
        )
    first[2].wait()
    pl.semaphore_wait(barrier, 1 + (n_x - 1) + h + m // max(h - 1, 1) * (h - 1))

    def to_pair(i, p, c):
        return remote(
            rows.at[i, part(slot[p], c), :],
            rows.at[i, pl.ds(pl.multiple_of(half + slot[p] * tok + c * pn.cut, pn.cut), pn.cut), :],
            sd.at[i, p, c],
            rd.at[i, p, c],
            partner,
        )

    def to_peer(i, k, c):
        r = rows.at[i, part(x, c), :]
        return remote(r, r, sx.at[i, k, c], rx.at[i, k, c], peers[k])

    def to_mate(k, c):
        r = part(x, c)
        return remote(
            rows.at[0, r, :], rows.at[h - k, r, :], s_own.at[k, c], rz.at[h - k, c],
            along(lax.rem(m + k, h)),
        )

    def to_cross(c):
        r = part(x, c)
        i = n_tp - 1 - m
        return remote(rows.at[0, r, :], rows.at[i, r, :], s_cross.at[c], rz.at[i, c], along(h))

    def to_member(i, k, c):
        r = rows.at[i, part(x, c), :]
        return remote(r, r, s_fwd.at[i - h, k, c], rz.at[i, c], along(lax.rem(m + k, h)))

    def share_peer(k):
        r = shr.at[0, x]
        return remote(r, r, share_x.at[0, k], share_x.at[1, k], peers[k])

    def share_pair(p):
        return remote(
            shr.at[0, slot[p]], shr.at[1, slot[p]], share_d.at[0, p], share_d.at[1, p], partner
        )

    def spread(i, c):
        for k in range(n_x - 1):
            send(to_peer(i, k, c))
        send(to_pair(i, 0, c))

    def from_line(i, c, log=sends):
        remote_wait = to_member(i, 1, c) if i >= h and h > 1 else None
        r = rows.at[i, part(x, c), :]
        copy = remote_wait or remote(r, r, s_cross.at[c], rz.at[i, c], along(h))
        copy.wait_recv()
        for k in range(n_x - 1):
            to_peer(i, k, c).start()
        to_pair(i, 0, c).start()

    def from_line_at(i, c, who):
        if who == "all":
            from_line(i, c)
        elif who == "gate":

            @pl.when(gate)
            def _():
                r = rows.at[i, part(x, c), :]
                remote(r, r, s_cross.at[c], rz.at[i, c], along(h)).wait_recv()
                for k in range(1, h):
                    to_member(i, k, c).start()
                for k in range(n_x - 1):
                    to_peer(i, k, c).start()
                to_pair(i, 0, c).start()

        elif h > 1:

            @pl.when(member)
            def _():
                from_line(i, c)

    def from_peers(i, c):
        for k in range(n_x - 1):
            to_peer(i, k, c).wait_recv()
            send(to_pair(i, n_x - 1 - k, c))

    for c in range(pn.cuts):
        for k in range(1, h):
            send(to_mate(k, c))
        spread(0, c)
    for c in range(pn.cuts):
        send(to_cross(c))
    for k in range(n_x - 1):
        send(share_peer(k))
    send(share_pair(0))

    arrivals = {s: [] for s in range(-1, n_tp)}
    for i in range(n_tp):
        if i >= h:
            arrivals[max(i - 3, -1)].append((0, i, "gate"))
        if i > 0:
            arrivals[max(i - 2, -1)].append((1 if i < h else 3, i, "all" if i < h else "member"))
        arrivals[i - 1].append((2, i, "peers"))

    def arrive(s, c):
        for _, i, who in sorted(arrivals[s], key=lambda a: (a[0] != 1, a[0], a[1])):
            if who == "peers":
                from_peers(i, c)
            else:
                from_line_at(i, c, who)

    for c in range(pn.cuts):
        arrive(-1, c)

    ngroups = pn.nt // pn.group
    groups_of = n_tp * ngroups
    for i in range(n_tp):
        for p in range(n_x):
            for c in range(pn.cuts):
                to_pair(i, p, c).wait_recv()
        if i == n_tp - 1:
            for k in range(n_x - 1):
                share_peer(k).wait_recv()
                send(share_pair(n_x - 1 - k))
            for p in range(n_x):
                share_pair(p).wait_recv()
            expert = me // (pn.n_exp // EXPERTS)
            eye = lax.broadcasted_iota(jnp.int32, (tok, tok), 0) == lax.broadcasted_iota(
                jnp.int32, (tok, tok), 1
            )
            for side_of in range(CORES):
                for p in range(n_x):
                    row = shr[side_of, p, pl.ds(expert, 1), 0:tok]
                    col = jnp.sum(
                        jnp.where(eye, jnp.broadcast_to(row, (tok, tok)), 0.0), axis=1, keepdims=True
                    )
                    at = side_of * half + p * tok
                    wcol[at : at + tok, :] = jnp.broadcast_to(col, (tok, 128))
        for g in range(ngroups):
            tiles = range(g * pn.group, (g + 1) * pn.group)
            for t in tiles:
                load(pn.at["gate", i, t]).wait()
                load(pn.at["up", i, t]).wait()
            for t in tiles:
                cols = slice(t * lanes, (t + 1) * lanes)
                a = rows[i]
                gv = jnp.dot(a, tile("gate", i, t), preferred_element_type=F32)
                uv = jnp.dot(a, tile("up", i, t), preferred_element_type=F32)
                if i > 0:
                    gv = gv + acc_g[:, cols]
                    uv = uv + acc_u[:, cols]
                if i < n_tp - 1:
                    acc_g[:, cols] = gv
                    acc_u[:, cols] = uv
                else:
                    hidden[:, cols] = (gv * jax.nn.sigmoid(gv) * uv * wcol[:, 0:1]).astype(BF16)
            start_loads(i * ngroups + g + 1)
            if i < n_tp - 1:
                for c in range(pn.cuts):
                    if min(c, ngroups - 1) == g or (g == ngroups - 1 and c >= ngroups):
                        arrive(i, c)

    n_pc = pn.n_pc
    n_cross = h * nq

    def pair_of(pc):
        return remote(psend.at[pc], precv.at[pc], pair2.at[0, pc], pair2.at[1, pc], partner)

    def x_of(pc, k):
        return remote(
            xsend.at[pc, k], xrecv.at[pc, k], x2.at[0, pc, k], x2.at[1, pc, k], peers[k]
        )

    def place(pc):
        return n_tp - 1 - pc // nq, pc % nq

    def to_gateway(pc):
        return remote(
            zsend.at[pc], grecv.at[m, pc], sz2.at[pc], rg2.at[m, pc], along(h - 1)
        )

    def from_member(mm, pc):
        return remote(
            zsend.at[pc], grecv.at[mm, pc], sz2.at[pc], rg2.at[mm, pc], along(h - 1)
        )

    def to_dest(pc):
        i, q = place(pc)
        r = 0 if i >= h else i
        return remote(zsend.at[pc], zrecv.at[r, q], sz2.at[pc], rz2.at[r, q], along(chunk(i)))

    def compute(pc):
        i, q = place(pc)
        for t in range(pw // lanes):
            n = q * (pw // lanes) + t
            load(pn.at["down", i, n]).wait()
            cols = slice(t * lanes, (t + 1) * lanes)
            p = jnp.dot(hidden[...], tile("down", i, n), preferred_element_type=F32)
            pown[pc, :, cols] = p[:half]
            psend[pc, :, cols] = p[half:].astype(BF16)
        start_loads(groups_of + pc + 1)
        send(pair_of(pc))

    def combine(pc):
        pair_of(pc).wait_recv()
        for k in range(n_x - 1):
            r = span(slot[k + 1])
            xsend[pc, k] = (pown[pc, r, :] + precv[pc, r, :].astype(F32)).astype(BF16)
            send(x_of(pc, k))

    def home(pc):
        i, q = place(pc)
        r = span(x)
        total = pown[pc, r, :] + precv[pc, r, :].astype(F32)
        for k in range(n_x - 1):
            x_of(pc, k).wait_recv()
            total = total + xrecv[pc, k].astype(F32)
        if i == 0:
            own[q] = total
        elif i < h:
            zsend[pc] = total.astype(BF16)
            send(to_dest(pc))
        else:
            if h > 1:

                @pl.when(member)
                def _():
                    zsend[pc] = total.astype(BF16)
                    to_gateway(pc).start()

            @pl.when(gate)
            def _():
                gsum[pc] = total

    def relay(pc):
        @pl.when(gate)
        def _():
            total = gsum[pc]
            for mm in range(h - 1):
                from_member(mm, pc).wait_recv()
                total = total + grecv[mm, pc].astype(F32)
            zsend[pc] = total.astype(BF16)
            to_dest(pc).start()

    for s in range(n_pc + max(LAG_PAIR, LAG_HOME, LAG_GATE)):
        if s < n_pc:
            compute(s)
        if 0 <= s - LAG_PAIR < n_pc:
            combine(s - LAG_PAIR)
        if 0 <= s - LAG_HOME < n_pc:
            home(s - LAG_HOME)
        if 0 <= s - LAG_GATE < n_cross:
            relay(s - LAG_GATE)
    for q in range(nq):
        total = own[q]
        for r in range(1, h):
            to_dest((n_tp - 1 - r) * nq + q).wait_recv()
            total = total + zrecv[r, q].astype(F32)
        to_dest(q).wait_recv()
        total = total + zrecv[0, q].astype(F32)
        out_ref[:, q * pw : (q + 1) * pw] = total.astype(BF16)

    for c in sends:
        c.wait_send()
    for i in range(1, n_tp):
        for c in range(pn.cuts):
            for k in range(n_x - 1):
                to_peer(i, k, c).wait_send()
            to_pair(i, 0, c).wait_send()
    for pc in range(n_cross):
        to_dest(pc).wait_send()

    @pl.when(gate)
    def _():
        for i in range(h, n_tp):
            for k in range(1, h):
                for c in range(pn.cuts):
                    to_member(i, k, c).wait_send()


def on_device(tokens, expert_ids, route_logits, gate_weight, up_weight, down_weight):
    n_exp = lax.axis_size("exp")
    n_tp = lax.axis_size("tp")
    tok, dc = tokens.shape
    width = gate_weight.shape[1]
    pn = Plan(n_exp, n_tp, tok, dc, width)
    n_x, h, half, nq, n_pc, pw = pn.n_x, pn.h, pn.half, pn.nq, pn.n_pc, pn.pw
    total = n_exp * tok
    mates = max(h - 1, 1)
    peers = max(n_x - 1, 1)
    dma = pltpu.SemaphoreType.DMA
    hbm = pl.BlockSpec(memory_space=pl.ANY)
    return pl.pallas_call(
        functools.partial(kernel, pn),
        out_shape=pltpu.VMEM((tok, dc), BF16),
        in_specs=[hbm] * 6,
        out_specs=pl.BlockSpec(memory_space=pltpu.VMEM),
        scratch_shapes=[
            pltpu.VMEM((pn.rows, pn.lanes), BF16),
            pltpu.VMEM((n_tp, total, dc), BF16),
            pltpu.VMEM((2, tok), jnp.int32),
            pltpu.VMEM((2, tok), F32),
            pltpu.VMEM((CORES, n_x, 8, 128), F32),
            pltpu.VMEM((total, 128), F32),
            pltpu.VMEM((total, width), F32),
            pltpu.VMEM((total, width), F32),
            pltpu.VMEM((total, width), BF16),
            pltpu.VMEM((n_pc, half, pw), F32),
            pltpu.VMEM((n_pc, half, pw), BF16),
            pltpu.VMEM((n_pc, half, pw), BF16),
            pltpu.VMEM((n_pc, peers, tok, pw), BF16),
            pltpu.VMEM((n_pc, peers, tok, pw), BF16),
            pltpu.VMEM((n_pc, tok, pw), BF16),
            pltpu.VMEM((mates, h * nq, tok, pw), BF16),
            pltpu.VMEM((h, nq, tok, pw), BF16),
            pltpu.VMEM((h * nq, tok, pw), F32),
            pltpu.VMEM((nq, tok, pw), F32),
            dma((len(pn.loads),)),
            dma((3,)),
            dma((n_tp, pn.cuts)),
            dma((n_tp, peers, pn.cuts)),
            dma((n_tp, n_x, pn.cuts)),
            dma((h, pn.cuts)),
            dma((pn.cuts,)),
            dma((h, h, pn.cuts)),
            dma((n_tp, peers, pn.cuts)),
            dma((n_tp, n_x, pn.cuts)),
            dma((2, peers)),
            dma((2, n_x)),
            dma((2, n_pc)),
            dma((2, n_pc, peers)),
            dma((n_pc,)),
            dma((mates, h * nq)),
            dma((h, nq)),
        ],
        compiler_params=pltpu.CompilerParams(
            collective_id=0, has_side_effects=True, vmem_limit_bytes=66500000
        ),
    )(tokens, expert_ids.T, route_logits.T, gate_weight, up_weight, down_weight)


def solution(mesh):
    return jax.shard_map(
        on_device,
        mesh=mesh,
        in_specs=(
            P(("rep", "exp"), "tp"),
            P(("rep", "exp"), None),
            P(("rep", "exp"), None),
            P(None, ("exp", "tp")),
            P(None, ("exp", "tp")),
            P(("exp", "tp"), None),
        ),
        out_specs=P(("rep", "exp"), "tp"),
        check_vma=False,
    )
```

time: 50.7 us -> 39.6 us (0.78)
  Pallas kernels: 48.9 us -> 38.8 us
  local copies, waits for them, and re-layouts: 1.54 us -> 0.64 us
    pallas_call x1, Pallas kernels: 48.9 us -> 38.8 us  [on_device(): pl.pallas_call(functools.partial(kernel, pn), out_shape=pltpu.VMEM((tok,...]
    unnamed x1, local copies, waits for them, and re-layouts: 1.54 us -> 0.64 us
where the time goes in v1:
time: 39.6 us; the launch traced here: 39.5 us
  Pallas kernels  38.8 us (98%)
  local copies, waits for them, and re-layouts  0.64 us (2%)
    pallas_call x1, Pallas kernels, on_device(): pl.pallas_call(functools.partial(kernel, pn), out_shape=pltpu.VMEM((tok,...  38.8 us

profile of v1, /device:TPU:0, one launch (start us, length us, event | category | flops | bytes accessed | tf_op | source)
XLA Modules:
  0.0 39.5 jit_solution(4568616802669164266)
XLA Ops:
  0.0 38.8 %shard_map.64 = bf16[32,1536]{1,0:T(8,128)(2,1)S(1)} custom-call(bf16[32,1536]{1,0:T(8,128)(2,1)} %tok_hbm.1, s32[2,32]{1,0:T(2,128)} %bitcast.2, f32[2,32]{1,0:T(2,128)} %bitcast.3, bf16[6144,2048]{1,0:T(8,128)(2,1)} %gate_hbm.1, bf16[6144,2048]{1,0:T(8,128)(2,1)} %up_hbm.1, bf16[2048,6144]{1,0:T(8,128)(2,1)} %down_hbm.1), custom_call_target="tpu_custom_call" | custom-call | tf_op jit(solution)/shard_map/pallas_call | solution.py:494
  38.8 0.6 %copy.8 = bf16[32,1536]{1,0:T(8,128)(2,1)} copy(bf16[32,1536]{1,0:T(8,128)(2,1)S(1)} %shard_map.64) | data formatting | bytes 196608
